TPU v7x, 32 devices: a whole 2x2x4 slice. The times are simulated.
32 devices in a mesh: rows: 8 (over z, x), grp: 4 (over y, core).
Axes of the slice: x: 2, y: 2, z: 4, core: 2. Of those that a mesh axis runs over, the one named last changes fastest.
Arguments:
- matrix: bfloat16 [10240, 16384], P(('rows', 'grp')), may hold values from -36 to 36
- sample_rows: int32 [32, 128, 256], P(('rows', 'grp')), may hold values from 0 to 319
- pair_list: int32 [8, 8, 4], replicated, may hold values from 0 to 255, as said below
- pair_count: int32 [8, 8], replicated, may hold values from 1 to 4, as said below
- pair_blocks: int32 [256, 2], replicated, may hold values from 0 to 127, as said below
Outputs:
- gram: float32 [256, 128, 128], P(('rows', 'grp'))
Inputs may be any that keep to these rules, and one draw needn't show every extreme that they name: `pair_list`: entry [s, r, k] lies in [r * 32, (r + 1) * 32); the 4 entries of one [s, r] are distinct. `pair_count`: every row group has some owner with all 4 slots active, and some owner has all 4 slots active from every row group. `pair_blocks`: the two blocks of a pair differ.
All inputs are finite; a program needn't handle non-finite values.
Results may differ from a plain program's by a relative error of at most 0.0016.
Values sent between devices are 32-bit elements; how exact they have to be, the bound alone decides.
No kernel may reach another device: no remote copies, remote signals or barrier semaphores. Data moves between devices by JAX's collectives and lax.ppermute only.
A program may use at most 192 MiB of HBM per device.

v0:
```python
import math
import jax
import jax.numpy as jnp
from jax import lax
from jax.sharding import PartitionSpec as P

epsilon = 1e-06


def shards(matrix, sample_rows, pair_list, pair_count, pair_blocks):
    rows_dev, column_count = matrix.shape
    block_count = sample_rows.shape[1]
    sample_count = sample_rows.shape[2]
    width = column_count // block_count
    row_axis_size = lax.axis_size("rows")
    grp_axis_size = lax.axis_size("grp")
    slot_cap = pair_list.shape[2]
    region_size = pair_blocks.shape[0] // row_axis_size
    row_index = lax.axis_index("rows")
    grp_index = lax.axis_index("grp")
    squares = jnp.sum(jnp.square(matrix.astype(jnp.float32)), axis=0)
    column_total = lax.psum(squares, ("rows", "grp"))
    root_mean = jnp.sqrt(column_total / (rows_dev * row_axis_size * grp_axis_size) + epsilon)
    positions = lax.iota(jnp.int32, rows_dev)
    picked = sample_rows[0]
    multiplicity = jnp.sum(
        (picked[:, :, None] == positions[None, None, :]).astype(jnp.float32), axis=1
    )
    blocks = matrix.reshape(rows_dev, block_count, width)
    weighted = (jnp.transpose(multiplicity)[:, :, None] * blocks.astype(jnp.float32)).astype(
        jnp.bfloat16
    )
    my_pairs = pair_list[row_index]
    my_counts = pair_count[row_index]
    live_mask = (lax.iota(jnp.int32, slot_cap)[None, :] < my_counts[:, None]).astype(jnp.float32)
    pair_ids = my_pairs.reshape(-1)
    slot_total = pair_ids.shape[0]
    group_size = math.gcd(32, slot_total)
    first_block = jnp.take(pair_blocks[:, 0], pair_ids).reshape(-1, group_size)
    second_block = jnp.take(pair_blocks[:, 1], pair_ids).reshape(-1, group_size)

    def tile_group(block_pair):
        weighted_cols = jnp.take(weighted, block_pair[0], axis=1)
        plain_cols = jnp.take(blocks, block_pair[1], axis=1)
        return jnp.einsum(
            "rgi,rgj->gij", weighted_cols, plain_cols, preferred_element_type=jnp.float32
        )

    partial_tiles = lax.map(tile_group, (first_block, second_block))
    partial_tiles = (
        partial_tiles.reshape(row_axis_size, slot_cap, width, width) * live_mask[:, :, None, None]
    )
    received = lax.all_to_all(partial_tiles, "rows", split_axis=0, concat_axis=0, tiled=True)
    source_ids = pair_list[:, row_index, :]
    local_ids = source_ids.reshape(-1) - row_index * region_size
    select_matrix = (lax.iota(jnp.int32, region_size)[:, None] == local_ids[None, :]).astype(
        jnp.float32
    )
    flat_received = received.reshape(local_ids.shape[0], width * width)
    owner_tiles = jnp.dot(
        select_matrix,
        flat_received,
        precision=lax.Precision.HIGHEST,
        preferred_element_type=jnp.float32,
    )
    owned_tiles = lax.psum_scatter(
        owner_tiles.reshape(region_size, width, width), "grp", scatter_dimension=0, tiled=True
    )
    tile_dev = owned_tiles.shape[0]
    owned_pairs = (row_index * grp_axis_size + grp_index) * tile_dev + lax.iota(jnp.int32, tile_dev)
    owned_blocks = jnp.take(pair_blocks, owned_pairs, axis=0)
    scale_blocks = root_mean.reshape(block_count, width)
    left_scale = jnp.take(scale_blocks, owned_blocks[:, 0], axis=0)
    right_scale = jnp.take(scale_blocks, owned_blocks[:, 1], axis=0)
    return owned_tiles / (sample_count * left_scale[:, :, None] * right_scale[:, None, :])


def solution(mesh):
    in_specs = (P(("rows", "grp"), None), P(("rows", "grp"), None, None), P(), P(), P())
    out_specs = P(("rows", "grp"), None, None)
    return jax.shard_map(shards, mesh=mesh, in_specs=in_specs, out_specs=out_specs, check_vma=False)
```

profile of v0, /device:TPU:1, one launch (start us, length us, event | category | flops | bytes accessed | tf_op | source)
XLA Modules:
  0.0 226.1 jit_solution(7144208598119614567)
XLA Ops:
  7.4 0.0 copy-start
  7.4 0.7 constant_dynamic-slice_fusion.1
  8.1 0.1 copy.22
  8.2 0.1 reshape_squeeze.4
  8.2 0.8 fusion.18
  9.0 0.7 gather_fusion.1
  9.7 0.7 gather_fusion.3
  10.4 9.4 %convert_reduce_fusion = f32[128,320]{1,0:T(8,128)S(1)} fusion(s32[128,256]{1,0:T(8,128)} %bitcast.48), kind=kLoop, calls=%fused_computation.7 | loop fusion | flops 31416320 | bytes 294912 | tf_op jit(solution)/shard_map/reduce_sum | solution.py:26
  19.8 11.0 %copy_bitcast_fusion = bf16[320,128,128]{2,0,1:T(8,128)(2,1)} fusion(bf16[320,16384]{1,0:T(8,128)(2,1)} %param.11), kind=kLoop, calls=%fused_computation.11 | loop fusion | bytes 20971520 | tf_op jit(solution)/shard_map/reshape | solution.py:29
  30.8 10.0 %multiply_convert_fusion = bf16[320,128,128]{2,0,1:T(8,128)(2,1)} fusion(f32[320,128]{0,1:T(8,128)S(1)} %bitcast.47, bf16[320,16384]{1,0:T(8,128)(2,1)} %param.11), kind=kLoop, calls=%fused_computation.10 | loop fusion | flops 15728640 | bytes 21135360 | tf_op jit(solution)/shard_map/convert_element_type | solution.py:30
  40.8 0.0 copy-done
  40.8 0.1 fusion.14
  40.9 5.0 %gather_fusion.2 = bf16[32,320,128]{2,1,0:T(8,128)(2,1)S(1)} fusion(bf16[320,128,128]{2,0,1:T(8,128)(2,1)} %multiply_convert_fusion, s32[1024]{0:T(1024)S(1)} %get-tuple-element.39), kind=kCustom, calls=%fused_computation.1.clone | custom fusion | bytes 5243008 | tf_op jit(solution)/shard_map/while/body/eval_jaxpr/jit(_take)/gather | solution.py:43
  45.9 6.4 %gather_fusion.4 = bf16[32,320,128]{2,1,0:T(8,128)(2,1)} fusion(bf16[320,128,128]{2,0,1:T(8,128)(2,1)} %copy_bitcast_fusion, s32[1024]{0:T(1024)S(1)} %get-tuple-element.38), kind=kCustom, calls=%fused_computation.4.clone | custom fusion | bytes 5243008 | tf_op jit(solution)/shard_map/while/body/eval_jaxpr/jit(_take)/gather | solution.py:44
  52.3 3.0 %fusion = f32[32,128,128]{2,1,0:T(8,128)S(1)} fusion(bf16[32,320,128]{2,1,0:T(8,128)(2,1)} %gather_fusion.4, bf16[32,320,128]{2,1,0:T(8,128)(2,1)S(1)} %gather_fusion.2, pred[32]{0:T(512)(128)(4,1)S(1)} %get-tuple-element.34, pred[32]{0:T(512)(128)(4,1)S(1)} %get-tuple-element.28), kind=kOutput, calls=%fused_computation.12 | convolution fusion | flops 338165760 | bytes 7340096 | tf_op jit(solution)/shard_map/while/body/eval_jaxpr/rgi,rgj->gij/dot_general | solution.py:45
  55.3 1.6 broadcast_multiply_fusion
  56.9 6.3 %all-to-all-start = ((f32[8,4,128,128]{3,2,1,0:T(8,128)}), f32[8,4,128,128]{3,2,1,0:T(8,128)S(1)}, u32[]{:S(2)}, u32[]{:S(2)}) async-start(f32[8,4,128,128]{3,2,1,0:T(8,128)} %broadcast_multiply_fusion), calls=%async_computation | async-start | bytes 4194304 | tf_op jit(solution)/shard_map/all_to_all | solution.py:53
  63.2 0.0 copy-start.1
  63.2 0.0 all-reduce.2.cloned.1.call-start
  63.3 6.8 %multiply_reduce_fusion = f32[16384]{0:T(1024)} fusion(bf16[320,16384]{1,0:T(8,128)(2,1)} %param.11), kind=kLoop, calls=%fused_computation.9 | loop fusion | flops 15712256 | bytes 10551296 | tf_op jit(solution)/shard_map/reduce_sum | solution.py:21
  70.0 0.0 all-reduce.2.cloned.1.call-update
  70.0 0.2 reduce-scatter.2.cloned.1.call-start
  70.3 0.0 copy-done.1
  70.3 0.3 subtract_reduce_fusion
  70.6 0.1 sub.15
  70.7 40.5 %all-to-all-done = f32[8,4,128,128]{3,2,1,0:T(8,128)S(1)} async-done(((f32[8,4,128,128]{3,2,1,0:T(8,128)}), f32[8,4,128,128]{3,2,1,0:T(8,128)S(1)}, u32[]{:S(2)}, u32[]{:S(2)}) %all-to-all-start) | async-done | bytes 2097184 | tf_op jit(solution)/shard_map/all_to_all | solution.py:53
  111.2 0.0 copy-start.2
  111.2 3.8 %fusion.7 = f32[32,128,128]{2,0,1:T(8,128)} fusion(s32[32]{0:T(128)S(1)} %sub.15, f32[4,8,128,128]{3,2,1,0:T(8,128)S(1)} %bitcast.45), kind=kOutput, calls=%fused_computation.20 | convolution fusion | flops 201327616 | bytes 4194432 | tf_op jit(solution)/shard_map/dot_general | solution.py:60
  114.9 0.0 reduce-scatter.2.cloned.1.call-update
  115.0 0.0 copy-done.2
  115.0 0.1 copy.26
  115.2 0.6 gather_fusion
  115.7 0.1 broadcast_select_fusion.1
  115.8 0.2 slice_reduce_fusion.1
  116.1 98.2 %all-reduce.2.cloned.1.call-done = f32[16384]{0:T(1024)} async-done(((f32[16384]{0:T(1024)}), f32[16384]{0:T(1024)}) %all-reduce.2.cloned.1.call-update) | async-done | bytes 65552 | tf_op jit(solution)/shard_map/psum | solution.py:22
  214.2 0.9 sqrt_bitcast_fusion
  215.1 0.6 gather_fusion.5
  215.7 0.1 select_multiply_fusion
  215.7 0.1 copy.27
  215.8 0.6 gather_fusion.6
  216.4 0.1 broadcast_select_fusion
  216.5 0.0 reduce-scatter.2.cloned.1.call-done
  216.5 1.2 multiply_divide_fusion
  217.7 0.9 copy.28
  (13 shorter events, 0.1 us)
Async XLA Ops:
  7.4 33.4 %copy-start = (s32[8,8]{1,0:T(8,128)S(1)}, s32[8,8]{1,0:T(8,128)}, u32[]{:S(2)}) copy-start(s32[8,8]{1,0:T(8,128)} %param.14) | copy-start | bytes 772
  56.9 54.3 %all-to-all-start = ((f32[8,4,128,128]{3,2,1,0:T(8,128)}), f32[8,4,128,128]{3,2,1,0:T(8,128)S(1)}, u32[]{:S(2)}, u32[]{:S(2)}) async-start(f32[8,4,128,128]{3,2,1,0:T(8,128)} %broadcast_multiply_fusion), calls=%async_computation | async-start | bytes 4194304 | tf_op jit(solution)/shard_map/all_to_all | solution.py:53
  63.2 7.1 %copy-start.1 = (s32[8,8,4]{1,2,0:T(4,128)S(1)}, s32[8,8,4]{1,2,0:T(4,128)}, u32[]{:S(2)}) copy-start(s32[8,8,4]{1,2,0:T(4,128)} %param.13) | copy-start | bytes 3076
  63.2 151.0 %all-reduce.2.cloned.1.call-start = ((), (), s32[]{:S(2)}) async-start(), calls=%async_computation.3 | async-start | bytes 131072 | tf_op jit(solution)/shard_map/psum | solution.py:22
  70.0 146.4 %reduce-scatter.2.cloned.1.call-start = ((), (), s32[]{:S(2)}) async-start(), calls=%async_computation.2 | async-start | bytes 2621440 | tf_op jit(solution)/shard_map/reduce_scatter | solution.py:66
  111.2 3.8 %copy-start.2 = (s32[256,2]{0,1:T(2,128)S(1)}, s32[256,2]{0,1:T(2,128)}, u32[]{:S(2)}) copy-start(s32[256,2]{0,1:T(2,128)} %param.15) | copy-start | bytes 6148
Sparse Core Ops, SparseCore 0:
  70.2 144.0 all-reduce.1
Sparse Core Ops, SparseCore 1:
  115.1 31.1 reduce-scatter.1
where the time goes:
time: 227 us; the launch traced here: 226 us
  waiting for transfers between devices  139 us (61%)
  other arithmetic  30.4 us (13%)
  local copies, waits for them, and re-layouts  28.5 us (13%)
  between operations  15 us (7%)
  matrix products  6.79 us (3%)
  starting transfers between devices  6.61 us (3%)
    psum x1, waiting for transfers between devices, shards(): column_total = lax.psum(squares, ('rows', 'grp'))  98.2 us
    all_to_all x1, waiting for transfers between devices, shards(): lax.all_to_all(partial_tiles, 'rows', split_axis=0, concat_axis=0, tiled=...  40.5 us
    reshape x1, local copies, waits for them, and re-layouts, shards(): blocks = matrix.reshape(rows_dev, block_count, width)  11 us
    convert_element_type x1, other arithmetic, shards(): (jnp.transpose(multiplicity)[:, :, None] * blocks.astype(jnp.float32)).as...  10 us
    reduce_sum x1, other arithmetic, shards(): jnp.sum((picked[:, :, None] == positions[None, None, :]).astype(jnp.float...  9.36 us
    reduce_sum x1, other arithmetic, shards(): squares = jnp.sum(jnp.square(matrix.astype(jnp.float32)), axis=0)  6.75 us
    gather x1, local copies, waits for them, and re-layouts, tile_group(): plain_cols = jnp.take(blocks, block_pair[1], axis=1)  6.38 us
    all_to_all x1, starting transfers between devices, shards(): lax.all_to_all(partial_tiles, 'rows', split_axis=0, concat_axis=0, tiled=...  6.34 us
  transfers between devices with their start and end apart: 3, of which 2 were waited for; matrix products, arithmetic and copies ran while one was open for 6% of the time, Pallas kernels for 0%

commit v1 on v0

--- a/solution.py
+++ b/solution.py
@@ -19,7 +19,7 @@
     row_index = lax.axis_index("rows")
     grp_index = lax.axis_index("grp")
     squares = jnp.sum(jnp.square(matrix.astype(jnp.float32)), axis=0)
-    column_total = lax.psum(squares, ("rows", "grp"))
+    column_total = jnp.sum(lax.all_gather(squares, ("rows", "grp")), axis=0)
     root_mean = jnp.sqrt(column_total / (rows_dev * row_axis_size * grp_axis_size) + epsilon)
     positions = lax.iota(jnp.int32, rows_dev)
     picked = sample_rows[0]

time: 227 us -> 161 us (0.71)
  waiting for transfers between devices: 139 us -> 73.6 us
    psum x1 -> x0, waiting for transfers between devices: 98.2 us -> none  [shards(): column_total = lax.psum(squares, ('rows', 'grp'))]
    reduce_scatter x1, waiting for transfers between devices: 0.01 us -> 26.7 us  [shards(): lax.psum_scatter(owner_tiles.reshape(region_size, width, width), 'grp', s...]
    all_to_all x1, waiting for transfers between devices: 40.5 us -> 46.9 us  [shards(): lax.all_to_all(partial_tiles, 'rows', split_axis=0, concat_axis=0, tiled=...]
  transfers between devices with their start and end apart: 3 -> 3, of which waited for: 2 -> 2; matrix products, arithmetic and copies ran while one was open for 6% -> 35% of each run, Pallas kernels for 0% -> 0%
where the time goes in v1:
time: 161 us; the launch traced here: 160 us
  waiting for transfers between devices  73.6 us (46%)
  local copies, waits for them, and re-layouts  28.8 us (18%)
  other arithmetic  28.8 us (18%)
  between operations  15.1 us (9%)
  matrix products  7.05 us (4%)
  starting transfers between devices  6.32 us (4%)
    all_to_all x1, waiting for transfers between devices, shards(): lax.all_to_all(partial_tiles, 'rows', split_axis=0, concat_axis=0, tiled=...  46.9 us
    reduce_scatter x1, waiting for transfers between devices, shards(): lax.psum_scatter(owner_tiles.reshape(region_size, width, width), 'grp', s...  26.7 us
    reshape x1, local copies, waits for them, and re-layouts, shards(): blocks = matrix.reshape(rows_dev, block_count, width)  11 us
    convert_element_type x1, other arithmetic, shards(): (jnp.transpose(multiplicity)[:, :, None] * blocks.astype(jnp.float32)).as...  9.97 us
    reduce_sum x1, other arithmetic, shards(): jnp.sum((picked[:, :, None] == positions[None, None, :]).astype(jnp.float...  8.39 us
    reduce_sum x1, other arithmetic, shards(): squares = jnp.sum(jnp.square(matrix.astype(jnp.float32)), axis=0)  6.76 us
    gather x1, local copies, waits for them, and re-layouts, tile_group(): plain_cols = jnp.take(blocks, block_pair[1], axis=1)  6.38 us
    all_to_all x1, starting transfers between devices, shards(): lax.all_to_all(partial_tiles, 'rows', split_axis=0, concat_axis=0, tiled=...  6.09 us
  transfers between devices with their start and end apart: 3, of which 2 were waited for; matrix products, arithmetic and copies ran while one was open for 35% of the time, Pallas kernels for 0%

profile of v1, /device:TPU:1, one launch (start us, length us, event | category | flops | bytes accessed | tf_op | source)
XLA Modules:
  0.0 159.7 jit_solution(10268728227132983596)
XLA Ops:
  7.4 0.0 copy-start
  7.4 0.0 all-gather.3.cloned.1.call-start
  7.4 6.8 %multiply_reduce_fusion = f32[16384]{0:T(1024)} fusion(bf16[320,16384]{1,0:T(8,128)(2,1)} %param.11), kind=kLoop, calls=%fused_computation.9 | loop fusion | flops 15712256 | bytes 10551296 | tf_op jit(solution)/shard_map/reduce_sum | solution.py:21
  14.1 0.0 all-gather.3.cloned.1.call-update
  14.2 0.0 copy-start.2
  14.2 0.0 copy-start.3
  14.2 0.0 copy-start.1
  14.2 11.0 %copy_bitcast_fusion = bf16[320,128,128]{2,0,1:T(8,128)(2,1)} fusion(bf16[320,16384]{1,0:T(8,128)(2,1)} %param.11), kind=kLoop, calls=%fused_computation.11 | loop fusion | bytes 20971520 | tf_op jit(solution)/shard_map/reshape | solution.py:29
  25.2 0.0 copy-done.2
  25.2 0.1 copy.29
  25.3 0.1 reshape_squeeze.4
  25.4 0.0 copy-done.3
  25.4 0.7 gather_fusion.1
  26.1 0.7 gather_fusion.3
  26.8 0.0 copy-done.1
  26.8 8.4 %convert_reduce_fusion = f32[128,320]{1,0:T(8,128)S(1)} fusion(s32[128,256]{1,0:T(8,128)S(1)} %bitcast.48), kind=kLoop, calls=%fused_computation.7 | loop fusion | flops 31416320 | bytes 294912 | tf_op jit(solution)/shard_map/reduce_sum | solution.py:26
  35.2 10.0 %multiply_convert_fusion = bf16[320,128,128]{2,0,1:T(8,128)(2,1)} fusion(f32[320,128]{0,1:T(8,128)S(1)} %bitcast.47, bf16[320,16384]{1,0:T(8,128)(2,1)} %param.11), kind=kLoop, calls=%fused_computation.10 | loop fusion | flops 15728640 | bytes 21135360 | tf_op jit(solution)/shard_map/convert_element_type | solution.py:30
  45.2 0.0 copy-done
  45.2 0.1 fusion.14
  45.3 5.0 %gather_fusion.2 = bf16[32,320,128]{2,1,0:T(8,128)(2,1)S(1)} fusion(bf16[320,128,128]{2,0,1:T(8,128)(2,1)} %multiply_convert_fusion, s32[1024]{0:T(1024)S(1)} %get-tuple-element.39), kind=kCustom, calls=%fused_computation.1.clone | custom fusion | bytes 5243008 | tf_op jit(solution)/shard_map/while/body/eval_jaxpr/jit(_take)/gather | solution.py:43
  50.4 6.4 %gather_fusion.4 = bf16[32,320,128]{2,1,0:T(8,128)(2,1)} fusion(bf16[320,128,128]{2,0,1:T(8,128)(2,1)} %copy_bitcast_fusion, s32[1024]{0:T(1024)S(1)} %get-tuple-element.38), kind=kCustom, calls=%fused_computation.4.clone | custom fusion | bytes 5243008 | tf_op jit(solution)/shard_map/while/body/eval_jaxpr/jit(_take)/gather | solution.py:44
  56.7 3.3 %fusion = f32[32,128,128]{2,1,0:T(8,128)S(1)} fusion(bf16[32,320,128]{2,1,0:T(8,128)(2,1)} %gather_fusion.4, bf16[32,320,128]{2,1,0:T(8,128)(2,1)S(1)} %gather_fusion.2, pred[32]{0:T(512)(128)(4,1)S(1)} %get-tuple-element.34, pred[32]{0:T(512)(128)(4,1)S(1)} %get-tuple-element.28), kind=kOutput, calls=%fused_computation.12 | convolution fusion | flops 338165760 | bytes 7340096 | tf_op jit(solution)/shard_map/while/body/eval_jaxpr/rgi,rgj->gij/dot_general | solution.py:45
  60.0 1.6 broadcast_multiply_fusion
  61.6 6.1 %all-to-all-start = ((f32[8,4,128,128]{3,2,1,0:T(8,128)}), f32[8,4,128,128]{3,2,1,0:T(8,128)S(1)}, u32[]{:S(2)}, u32[]{:S(2)}) async-start(f32[8,4,128,128]{3,2,1,0:T(8,128)} %broadcast_multiply_fusion), calls=%async_computation | async-start | bytes 4194304 | tf_op jit(solution)/shard_map/all_to_all | solution.py:53
  67.7 0.2 reduce-scatter.2.cloned.1.call-start
  67.9 0.3 subtract_reduce_fusion
  68.2 0.1 sub.15
  68.3 46.9 %all-to-all-done = f32[8,4,128,128]{3,2,1,0:T(8,128)S(1)} async-done(((f32[8,4,128,128]{3,2,1,0:T(8,128)}), f32[8,4,128,128]{3,2,1,0:T(8,128)S(1)}, u32[]{:S(2)}, u32[]{:S(2)}) %all-to-all-start) | async-done | bytes 2097184 | tf_op jit(solution)/shard_map/all_to_all | solution.py:53
  115.1 3.8 %fusion.7 = f32[32,128,128]{2,0,1:T(8,128)} fusion(s32[32]{0:T(128)S(1)} %sub.15, f32[4,8,128,128]{3,2,1,0:T(8,128)S(1)} %bitcast.45), kind=kOutput, calls=%fused_computation.20 | convolution fusion | flops 201327616 | bytes 4194432 | tf_op jit(solution)/shard_map/dot_general | solution.py:60
  118.9 0.0 reduce-scatter.2.cloned.1.call-update
  118.9 0.1 copy.33
  119.1 0.6 gather_fusion
  119.7 0.1 broadcast_select_fusion.1
  119.8 0.2 slice_reduce_fusion.1
  120.0 0.0 all-gather.3.cloned.1.call-done
  120.0 1.8 %reshape.157 = f32[32,16384]{1,0:T(8,128)S(1)} reshape(f32[524288]{0:T(1024)} %all-gather.3.cloned.1.call-done) | data formatting | bytes 4194304 | tf_op jit(solution)/shard_map/all_gather | solution.py:22
  121.8 0.2 reduce_sum.29
  122.0 0.6 gather_fusion.5
  122.6 0.1 select_multiply_fusion
  122.7 0.1 copy.34
  122.8 0.6 gather_fusion.6
  123.3 0.1 broadcast_select_fusion
  123.4 26.7 %reduce-scatter.2.cloned.1.call-done = f32[8,128,128]{2,0,1:T(8,128)} async-done(((f32[32,128,128]{2,0,1:T(8,128)}), f32[8,128,128]{2,0,1:T(8,128)}) %reduce-scatter.2.cloned.1.call-update) | async-done | bytes 524304 | tf_op jit(solution)/shard_map/reduce_scatter | solution.py:66
  150.1 1.2 multiply_divide_fusion
  151.3 0.9 copy.35
  (16 shorter events, 0.1 us)
Async XLA Ops:
  7.4 37.8 %copy-start = (s32[8,8]{1,0:T(8,128)S(1)}, s32[8,8]{1,0:T(8,128)}, u32[]{:S(2)}) copy-start(s32[8,8]{1,0:T(8,128)} %param.14) | copy-start | bytes 772
  7.4 112.7 %all-gather.3.cloned.1.call-start = ((), (), s32[]{:S(2)}) async-start(), calls=%async_computation.3 | async-start | bytes 2162688 | tf_op jit(solution)/shard_map/all_gather | solution.py:22
  14.2 11.0 %copy-start.2 = (s32[8,8,4]{1,2,0:T(4,128)S(1)}, s32[8,8,4]{1,2,0:T(4,128)}, u32[]{:S(2)}) copy-start(s32[8,8,4]{1,2,0:T(4,128)} %param.13) | copy-start | bytes 3076
  14.2 11.2 %copy-start.3 = (s32[256,2]{0,1:T(2,128)S(1)}, s32[256,2]{0,1:T(2,128)}, u32[]{:S(2)}) copy-start(s32[256,2]{0,1:T(2,128)} %param.15) | copy-start | bytes 6148
  14.2 12.6 %copy-start.1 = (s32[1,128,256]{2,1,0:T(8,128)S(1)}, s32[1,128,256]{2,1,0:T(8,128)}, u32[]{:S(2)}) copy-start(s32[1,128,256]{2,1,0:T(8,128)} %param.12) | copy-start | bytes 393220
  61.6 53.6 %all-to-all-start = ((f32[8,4,128,128]{3,2,1,0:T(8,128)}), f32[8,4,128,128]{3,2,1,0:T(8,128)S(1)}, u32[]{:S(2)}, u32[]{:S(2)}) async-start(f32[8,4,128,128]{3,2,1,0:T(8,128)} %broadcast_multiply_fusion), calls=%async_computation | async-start | bytes 4194304 | tf_op jit(solution)/shard_map/all_to_all | solution.py:53
  67.7 82.4 %reduce-scatter.2.cloned.1.call-start = ((), (), s32[]{:S(2)}) async-start(), calls=%async_computation.2 | async-start | bytes 2621440 | tf_op jit(solution)/shard_map/reduce_scatter | solution.py:66
Sparse Core Ops, SparseCore 0:
  14.3 58.7 all-gather.2
Sparse Core Ops, SparseCore 1:
  119.0 31.0 reduce-scatter.1
